TPU v7x, 32 devices: a whole 2x2x4 slice. The times are simulated.
32 devices in a mesh: section: 2 (over x), tensor: 8 (over z, core), dp: 2 (over y).
Axes of the slice: x: 2, y: 2, z: 4, core: 2. Of those that a mesh axis runs over, the one named last changes fastest.
Arguments:
- dec_queries: bfloat16 [2, 4, 512, 8192], P('section', 'dp', None, 'tensor'), may hold values from -8 to 8
- enc_keys: bfloat16 [2, 4, 512, 8192], P('section', 'dp', None, 'tensor'), may hold values from -4 to 4
- enc_values: bfloat16 [2, 4, 512, 8192], P('section', 'dp', None, 'tensor'), may hold values from -4 to 4
- out_grad: bfloat16 [2, 4, 512, 8192], P('section', 'dp', None, 'tensor'), may hold values from -15 to 15
- key_weight: bfloat16 [2, 1024, 8192], P('section', None, 'tensor'), may hold values from -0.1875 to 0.1875
- value_weight: bfloat16 [2, 1024, 8192], P('section', None, 'tensor'), may hold values from -0.1875 to 0.1875
- enc_hidden: float32 [4, 512, 1024], P('dp', 'section', 'tensor'), may hold values from -2 to 2, as said below
- enc_gain: float32 [1024], P('tensor'), may hold values from 0.1 to 1.9
Outputs:
- enc_input_grad: float32 [4, 512, 1024], P('dp', 'section', 'tensor')
Inputs may be any that keep to these rules, and one draw needn't show every extreme that they name: `enc_hidden`: every entry's magnitude is at least 0.25.
All inputs are finite; a program needn't handle non-finite values.
Results may differ from a plain program's by a relative error of at most 0.0041.
Values sent between devices are 32-bit elements; how exact they have to be, the bound alone decides.
A program may use at most 128 MiB of HBM per device.

v0:
```python
import jax
import jax.numpy as jnp
from jax import lax
from jax.sharding import PartitionSpec as P

D = 1024
DK = 128
epsilon = 1e-06


def per_device(
    dec_queries, enc_keys, enc_values, out_grad, key_weight, value_weight, enc_hidden, enc_gain
):
    seqs_here = dec_queries.shape[1]
    dec_len = dec_queries.shape[2]
    hidden_here = dec_queries.shape[3]
    enc_len = enc_keys.shape[2]
    heads_here = hidden_here // DK
    model_width = key_weight.shape[1]
    square_total = lax.psum(jnp.sum(enc_hidden * enc_hidden, axis=-1), "tensor")
    query_heads = dec_queries[0].reshape(seqs_here, dec_len, heads_here, DK)
    key_heads = enc_keys[0].reshape(seqs_here, enc_len, heads_here, DK)
    value_heads = enc_values[0].reshape(seqs_here, enc_len, heads_here, DK)
    grad_heads = out_grad[0].reshape(seqs_here, dec_len, heads_here, DK)
    scores = jnp.einsum(
        "bqhd,bkhd->bhqk", query_heads, key_heads, preferred_element_type=jnp.float32
    )
    shifted = jnp.exp(scores - jnp.max(scores, axis=-1, keepdims=True))
    attn_probs = shifted / jnp.sum(shifted, axis=-1, keepdims=True)
    probs_low = attn_probs.astype(jnp.bfloat16)
    attended = jnp.einsum(
        "bhqk,bkhd->bqhd", probs_low, value_heads, preferred_element_type=jnp.float32
    )
    row_dot = jnp.sum(grad_heads.astype(jnp.float32) * attended, axis=-1)
    value_grad = jnp.einsum(
        "bhqk,bqhd->bkhd", probs_low, grad_heads, preferred_element_type=jnp.float32
    ).astype(jnp.bfloat16)
    prob_grad = jnp.einsum(
        "bqhd,bkhd->bhqk", grad_heads, value_heads, preferred_element_type=jnp.float32
    )
    score_low = (attn_probs * (prob_grad - jnp.transpose(row_dot, (0, 2, 1))[..., None])).astype(
        jnp.bfloat16
    )
    key_grad = jnp.einsum(
        "bhqk,bqhd->bkhd", score_low, query_heads, preferred_element_type=jnp.float32
    ).astype(jnp.bfloat16)
    flat_rows = seqs_here * enc_len
    partial_value = jnp.einsum(
        "th,dh->td",
        key_grad.reshape(flat_rows, hidden_here),
        key_weight[0],
        preferred_element_type=jnp.float32,
    )
    partial_value = partial_value + jnp.einsum(
        "th,dh->td",
        value_grad.reshape(flat_rows, hidden_here),
        value_weight[0],
        preferred_element_type=jnp.float32,
    )
    partial_value = partial_value.reshape(seqs_here, enc_len, model_width)
    head_part = lax.psum_scatter(partial_value, "tensor", scatter_dimension=2, tiled=True)
    enc_grad = lax.psum_scatter(head_part, "section", scatter_dimension=1, tiled=True)
    scaled = enc_gain * enc_grad
    cross_local = jnp.sum(scaled * enc_hidden, axis=-1)
    cross_total = lax.psum(cross_local, "tensor")
    inverse = lax.rsqrt(square_total / D + epsilon)
    return (
        scaled * inverse[..., None]
        - enc_hidden * (cross_total * inverse * inverse * inverse / D)[..., None]
    )


def solution(mesh):
    return jax.shard_map(
        per_device,
        mesh=mesh,
        in_specs=(
            P("section", "dp", None, "tensor"),
            P("section", "dp", None, "tensor"),
            P("section", "dp", None, "tensor"),
            P("section", "dp", None, "tensor"),
            P("section", None, "tensor"),
            P("section", None, "tensor"),
            P("dp", "section", "tensor"),
            P("tensor"),
        ),
        out_specs=P("dp", "section", "tensor"),
        check_vma=False,
    )
```

profile of v0, /device:TPU:0, one launch (start us, length us, event | category | flops | bytes accessed | tf_op | source)
XLA Modules:
  0.0 159.6 jit_solution(9555363609104835648)
XLA Ops:
  6.5 0.0 reduce-scatter.3.cloned.1.call-start
  6.5 3.7 %copy.40 = bf16[128,8,8,128]{3,2,1,0:T(8,128)(2,1)} copy(bf16[128,8,8,128]{3,1,2,0:T(8,128)(2,1)} %bitcast.55) | data formatting | bytes 4194304
  10.3 2.0 %copy.41 = bf16[128,8,8,128]{3,2,1,0:T(8,128)(2,1)} copy(bf16[128,8,8,128]{3,1,2,0:T(8,128)(2,1)S(1)} %bitcast.56) | data formatting | bytes 4194304
  12.2 3.9 %copy.39 = bf16[1,2,512,1024]{2,3,1,0:T(8,128)(2,1)} copy(bf16[1,2,512,1024]{3,2,1,0:T(8,128)(2,1)} %param.10) | data formatting | bytes 4194304 | tf_op jit(solution)/shard_map/reshape;squeeze | solution.py:23
  16.2 3.9 %copy.21 = bf16[1,2,512,1024]{2,3,1,0:T(8,128)(2,1)} copy(bf16[1,2,512,1024]{3,2,1,0:T(8,128)(2,1)} %param.11) | data formatting | bytes 4194304 | tf_op args[3]
  20.1 10.7 %fusion.29 = (f32[2,8,512]{2,1,0:T(8,128)S(1)}, f32[2,8,512,512]{2,3,1,0:T(8,128)}) fusion(bf16[2,512,8,128]{3,2,1,0:T(8,128)(2,1)} %bitcast.60, bf16[2,512,8,128]{3,2,1,0:T(8,128)(2,1)} %bitcast.57), kind=kOutput, calls=%fused_computation.31 | convolution fusion | flops 1082130944 | bytes 21004288 | tf_op jit(solution)/shard_map/sub | solution.py:28
  30.8 6.8 %fusion.3 = bf16[2,8,512,512]{2,3,1,0:T(8,128)(2,1)S(1)} fusion(f32[2,8,512,512]{2,3,1,0:T(8,128)} %get-tuple-element.12, f32[2,8,512]{2,1,0:T(8,128)S(1)} %get-tuple-element.11), kind=kLoop, calls=%fused_computation.6 | loop fusion | flops 8388608 | bytes 25198592 | tf_op jit(solution)/shard_map/convert_element_type | solution.py:30
  37.6 2.3 %convert_bitcast_fusion = bf16[2,512,8,128]{3,1,2,0:T(8,128)(2,1)S(1)} fusion(bf16[2,8,512,512]{2,3,1,0:T(8,128)(2,1)S(1)} %fusion.3, bf16[2,512,8,128]{1,3,2,0:T(8,128)(2,1)S(1)} %bitcast.52), kind=kOutput, calls=%fused_computation.20 | convolution fusion | flops 1074790400 | bytes 12582912 | tf_op jit(solution)/shard_map/bhqk,bqhd->bkhd/dot_general | solution.py:35
  40.0 0.0 copy-done.1
  40.0 1.3 fusion.6
  41.3 2.7 %copy.32 = bf16[2,512,8,128]{3,2,1,0:T(8,128)(2,1)} copy(bf16[2,512,8,128]{3,1,2,0:T(8,128)(2,1)S(1)} %convert_bitcast_fusion) | data formatting | bytes 4194304 | tf_op jit(solution)/shard_map/convert_element_type | solution.py:37
  44.0 11.6 %convert_bitcast_fusion.1 = bf16[2,512,8,128]{3,1,2,0:T(8,128)(2,1)} fusion(f32[2,8,512]{2,1,0:T(8,128)S(1)} %bitcast.62, f32[2,8,512,512]{2,3,1,0:T(8,128)} %get-tuple-element.12, f32[2,8,512]{2,1,0:T(8,128)S(1)} %get-tuple-element.11, bf16[2,512,8,128]{1,3,2,0:T(8,128)(2,1)} %bitcast.49, bf16[2,512,8,128]{1,3,2,0:T(8,128)(2,1)} %bitcast.51, ...), kind=kOutput, calls=%fused_computation.21 | convolution fusion | flops 2165309440 | bytes 25231360 | tf_op jit(solution)/shard_map/bhqk,bqhd->bkhd/dot_general | solution.py:44
  55.5 3.1 %copy.30 = bf16[2,512,8,128]{3,2,1,0:T(8,128)(2,1)S(1)} copy(bf16[2,512,8,128]{3,1,2,0:T(8,128)(2,1)} %convert_bitcast_fusion.1) | data formatting | bytes 4194304 | tf_op jit(solution)/shard_map/convert_element_type | solution.py:46
  58.7 0.0 copy-start.7
  58.7 2.4 %fusion.7 = f32[1024,1024]{1,0:T(8,128)S(1)} fusion(bf16[128,8,8,128]{3,2,1,0:T(8,128)(2,1)S(1)} %bitcast.59, bf16[1,1024,1024]{2,1,0:T(8,128)(2,1)S(1)} %copy-done), kind=kOutput, calls=%fused_computation.10 | convolution fusion | flops 2147483648 | bytes 8388608 | tf_op jit(solution)/shard_map/th,dh->td/dot_general | solution.py:54
  61.1 4.3 %fusion.17 = f32[1024,1024]{1,0:T(8,128)} fusion(f32[1024,1024]{1,0:T(8,128)S(1)} %fusion.7, bf16[1,1024,1024]{2,1,0:T(8,128)(2,1)S(1)} %copy-done.7, bf16[128,8,8,128]{3,2,1,0:T(8,128)(2,1)S(1)} %bitcast.61), kind=kOutput, calls=%fused_computation.22 | convolution fusion | flops 2148532224 | bytes 12582912 | tf_op jit(solution)/shard_map/th,dh->td/dot_general | solution.py:48
  65.3 0.0 reduce-scatter.3.cloned.1.call-update
  65.4 0.0 reduce-scatter.5.cloned.1.call-start
  65.4 52.8 %reduce-scatter.3.cloned.1.call-done = f32[2,512,128]{2,1,0:T(8,128)} async-done(((f32[2,512,1024]{2,1,0:T(8,128)}), f32[2,512,128]{2,1,0:T(8,128)}) %reduce-scatter.3.cloned.1.call-update) | async-done | bytes 524304 | tf_op jit(solution)/shard_map/reduce_scatter | solution.py:61
  118.2 0.0 reduce-scatter.5.cloned.1.call-update
  118.2 15.4 %reduce-scatter.5.cloned.1.call-done = f32[2,256,128]{2,1,0:T(8,128)} async-done(((f32[2,512,128]{2,1,0:T(8,128)}), f32[2,256,128]{2,1,0:T(8,128)}) %reduce-scatter.5.cloned.1.call-update) | async-done | bytes 262160 | tf_op jit(solution)/shard_map/reduce_scatter | solution.py:62
  133.6 1.2 multiply_reduce_fusion.1
  134.7 16.2 %all-reduce = (f32[2,256]{1,0:T(2,128)S(1)}, f32[2,256]{1,0:T(2,128)S(1)}) all-reduce(f32[2,256]{1,0:T(2,128)S(1)} %get-tuple-element.6, f32[2,256]{1,0:T(2,128)S(1)} %get-tuple-element.5), channel_id=1, replica_groups=mesh['section'=2,'tensor'=8,'dp'=2] {'tensor'}, use_global_device_ids=true, to_apply=%region_8.0 | all-reduce | flops 1024 | bytes 8192 | tf_op jit(solution)/shard_map/psum | solution.py:65
  150.9 1.9 %multiply_subtract_fusion = f32[2,256,128]{2,1,0:T(8,128)} fusion(f32[2,256,128]{2,1,0:T(8,128)S(1)} %copy-done.5, f32[2,256,128]{2,1,0:T(8,128)} %reduce-scatter.5.cloned.1.call-done, f32[2,256]{1,0:T(2,128)S(1)} %get-tuple-element.10, f32[2,256]{1,0:T(2,128)S(1)} %get-tuple-element.9, f32[128]{0:T(128)S(1)} %copy-done.6), kind=kLoop, calls=%fused_computation.25 | loop fusion | flops 262144 | bytes 791040 | tf_op jit(solution)/shard_map/sub | solution.py:68
  (15 shorter events, 0.0 us)
Async XLA Ops:
  6.5 52.1 %copy-start = (bf16[1,1024,1024]{2,1,0:T(8,128)(2,1)S(1)}, bf16[1,1024,1024]{2,1,0:T(8,128)(2,1)}, u32[]{:S(2)}) copy-start(bf16[1,1024,1024]{2,1,0:T(8,128)(2,1)} %param.13) | copy-start | bytes 6291460
  6.5 111.6 %reduce-scatter.3.cloned.1.call-start = ((), (), s32[]{:S(2)}) async-start(), calls=%async_computation.2 | async-start | bytes 4718592 | tf_op jit(solution)/shard_map/reduce_scatter | solution.py:61
  6.5 3.7 %copy-start.3 = (bf16[1,2,512,1024]{3,2,1,0:T(8,128)(2,1)S(1)}, bf16[1,2,512,1024]{3,2,1,0:T(8,128)(2,1)}, u32[]{:S(2)}) copy-start(bf16[1,2,512,1024]{3,2,1,0:T(8,128)(2,1)} %param.9) | copy-start | bytes 6291460
  30.8 6.9 %copy-start.2 = (bf16[1,2,512,1024]{2,3,1,0:T(8,128)(2,1)S(1)}, bf16[1,2,512,1024]{2,3,1,0:T(8,128)(2,1)}, u32[]{:S(2)}) copy-start(bf16[1,2,512,1024]{2,3,1,0:T(8,128)(2,1)} %copy.21) | copy-start | bytes 6291460
  37.6 2.4 %copy-start.1 = (bf16[1,2,512,1024]{2,3,1,0:T(8,128)(2,1)S(1)}, bf16[1,2,512,1024]{2,3,1,0:T(8,128)(2,1)}, u32[]{:S(2)}) copy-start(bf16[1,2,512,1024]{2,3,1,0:T(8,128)(2,1)} %copy.39) | copy-start | bytes 6291460
  55.5 3.1 %copy-start.4 = (bf16[2,512,8,128]{3,2,1,0:T(8,128)(2,1)S(1)}, bf16[2,512,8,128]{3,2,1,0:T(8,128)(2,1)}, u32[]{:S(2)}) copy-start(bf16[2,512,8,128]{3,2,1,0:T(8,128)(2,1)} %copy.32) | copy-start | bytes 6291460
  58.7 2.4 %copy-start.7 = (bf16[1,1024,1024]{2,1,0:T(8,128)(2,1)S(1)}, bf16[1,1024,1024]{2,1,0:T(8,128)(2,1)}, u32[]{:S(2)}) copy-start(bf16[1,1024,1024]{2,1,0:T(8,128)(2,1)} %param.12) | copy-start | bytes 6291460
  65.3 68.2 %copy-start.5 = (f32[2,256,128]{2,1,0:T(8,128)S(1)}, f32[2,256,128]{2,1,0:T(8,128)}, u32[]{:S(2)}) copy-start(f32[2,256,128]{2,1,0:T(8,128)} %param.14) | copy-start | bytes 786436
  65.3 68.2 %copy-start.6 = (f32[128]{0:T(128)S(1)}, f32[128]{0:T(128)}, u32[]{:S(2)}) copy-start(f32[128]{0:T(128)} %param.15) | copy-start | bytes 1540
  65.4 68.2 %reduce-scatter.5.cloned.1.call-start = ((), (), s32[]{:S(2)}) async-start(), calls=%async_computation.3 | async-start | bytes 786432 | tf_op jit(solution)/shard_map/reduce_scatter | solution.py:62
Sparse Core Ops, SparseCore 0:
  65.5 52.6 reduce-scatter.2
  120.4 13.0 reduce-scatter.4
where the time goes:
time: 160 us
  waiting for transfers between devices  68.1 us (43%)
  matrix products  32.5 us (20%)
  local copies, waits for them, and re-layouts  19.4 us (12%)
  blocking collectives  16.2 us (10%)
  between operations  13.5 us (8%)
  other arithmetic  9.88 us (6%)
    reduce_scatter x1, waiting for transfers between devices, per_device(): lax.psum_scatter(partial_value, 'tensor', scatter_dimension=2, tiled=True)  52.8 us
    psum x1, blocking collectives, per_device(): cross_total = lax.psum(cross_local, 'tensor')  16.2 us
    reduce_scatter x1, waiting for transfers between devices, per_device(): lax.psum_scatter(head_part, 'section', scatter_dimension=1, tiled=True)  15.4 us
    dot_general x1, matrix products, per_device(): jnp.einsum('bhqk,bqhd->bkhd', score_low, query_heads, preferred_element_t...  11.6 us
    sub x1, matrix products, per_device(): shifted = jnp.exp(scores - jnp.max(scores, axis=-1, keepdims=True))  10.7 us
    unnamed x19, local copies, waits for them, and re-layouts  9.66 us
    convert_element_type x1, other arithmetic, per_device(): probs_low = attn_probs.astype(jnp.bfloat16)  6.84 us
    dot_general x1, matrix products, per_device(): jnp.einsum('th,dh->td', key_grad.reshape(flat_rows, hidden_here), key_wei...  4.29 us
  transfers between devices with their start and end apart: 2, of which 2 were waited for; matrix products, arithmetic and copies ran while one was open for 0% of the time, Pallas kernels for 0%

commit v1 on v0

--- a/solution.py
+++ b/solution.py
@@ -62,7 +62,7 @@
     enc_grad = lax.psum_scatter(head_part, "section", scatter_dimension=1, tiled=True)
     scaled = enc_gain * enc_grad
     cross_local = jnp.sum(scaled * enc_hidden, axis=-1)
-    cross_total = lax.psum(cross_local, "tensor")
+    cross_total = jnp.sum(lax.all_gather(cross_local, "tensor"), axis=0)
     inverse = lax.rsqrt(square_total / D + epsilon)
     return (
         scaled * inverse[..., None]

time: 160 us -> 173 us (1.081)
  blocking collectives: 16.2 us -> 29 us
    all_gather x0 -> x1, blocking collectives: none -> 12.8 us  [per_device(): cross_total = jnp.sum(lax.all_gather(cross_local, 'tensor'), axis=0)]
where the time goes in v1:
time: 173 us; the launch traced here: 172 us
  waiting for transfers between devices  68.1 us (39%)
  matrix products  32.5 us (19%)
  blocking collectives  29 us (17%)
  local copies, waits for them, and re-layouts  19.4 us (11%)
  between operations  13.5 us (8%)
  other arithmetic  9.9 us (6%)
    reduce_scatter x1, waiting for transfers between devices, per_device(): lax.psum_scatter(partial_value, 'tensor', scatter_dimension=2, tiled=True)  52.8 us
    psum x1, blocking collectives, per_device(): square_total = lax.psum(jnp.sum(enc_hidden * enc_hidden, axis=-1), 'tensor')  16.2 us
    reduce_scatter x1, waiting for transfers between devices, per_device(): lax.psum_scatter(head_part, 'section', scatter_dimension=1, tiled=True)  15.4 us
    all_gather x1, blocking collectives, per_device(): cross_total = jnp.sum(lax.all_gather(cross_local, 'tensor'), axis=0)  12.8 us
    dot_general x1, matrix products, per_device(): jnp.einsum('bhqk,bqhd->bkhd', score_low, query_heads, preferred_element_t...  11.6 us
    sub x1, matrix products, per_device(): shifted = jnp.exp(scores - jnp.max(scores, axis=-1, keepdims=True))  10.7 us
    unnamed x19, local copies, waits for them, and re-layouts  9.66 us
    convert_element_type x1, other arithmetic, per_device(): probs_low = attn_probs.astype(jnp.bfloat16)  6.84 us
  transfers between devices with their start and end apart: 2, of which 2 were waited for; matrix products, arithmetic and copies ran while one was open for 0% of the time, Pallas kernels for 0%

profile of v1, /device:TPU:0, one launch (start us, length us, event | category | flops | bytes accessed | tf_op | source)
XLA Modules:
  0.0 172.4 jit_solution(14212311878776878342)
XLA Ops:
  6.5 0.0 reduce-scatter.3.cloned.1.call-start
  6.5 3.7 %copy.40 = bf16[128,8,8,128]{3,2,1,0:T(8,128)(2,1)} copy(bf16[128,8,8,128]{3,1,2,0:T(8,128)(2,1)} %bitcast.56) | data formatting | bytes 4194304
  10.3 2.0 %copy.41 = bf16[128,8,8,128]{3,2,1,0:T(8,128)(2,1)} copy(bf16[128,8,8,128]{3,1,2,0:T(8,128)(2,1)S(1)} %bitcast.57) | data formatting | bytes 4194304
  12.2 3.9 %copy.39 = bf16[1,2,512,1024]{2,3,1,0:T(8,128)(2,1)} copy(bf16[1,2,512,1024]{3,2,1,0:T(8,128)(2,1)} %param.10) | data formatting | bytes 4194304 | tf_op jit(solution)/shard_map/reshape;squeeze | solution.py:23
  16.2 3.9 %copy.21 = bf16[1,2,512,1024]{2,3,1,0:T(8,128)(2,1)} copy(bf16[1,2,512,1024]{3,2,1,0:T(8,128)(2,1)} %param.11) | data formatting | bytes 4194304 | tf_op args[3]
  20.1 10.7 %fusion.29 = (f32[2,8,512]{2,1,0:T(8,128)S(1)}, f32[2,8,512,512]{2,3,1,0:T(8,128)}) fusion(bf16[2,512,8,128]{3,2,1,0:T(8,128)(2,1)} %bitcast.61, bf16[2,512,8,128]{3,2,1,0:T(8,128)(2,1)} %bitcast.58), kind=kOutput, calls=%fused_computation.31 | convolution fusion | flops 1082130944 | bytes 21004288 | tf_op jit(solution)/shard_map/sub | solution.py:28
  30.8 6.8 %fusion.3 = bf16[2,8,512,512]{2,3,1,0:T(8,128)(2,1)S(1)} fusion(f32[2,8,512,512]{2,3,1,0:T(8,128)} %get-tuple-element.10, f32[2,8,512]{2,1,0:T(8,128)S(1)} %get-tuple-element.9), kind=kLoop, calls=%fused_computation.6 | loop fusion | flops 8388608 | bytes 25198592 | tf_op jit(solution)/shard_map/convert_element_type | solution.py:30
  37.6 2.3 %convert_bitcast_fusion = bf16[2,512,8,128]{3,1,2,0:T(8,128)(2,1)S(1)} fusion(bf16[2,8,512,512]{2,3,1,0:T(8,128)(2,1)S(1)} %fusion.3, bf16[2,512,8,128]{1,3,2,0:T(8,128)(2,1)S(1)} %bitcast.53), kind=kOutput, calls=%fused_computation.20 | convolution fusion | flops 1074790400 | bytes 12582912 | tf_op jit(solution)/shard_map/bhqk,bqhd->bkhd/dot_general | solution.py:35
  40.0 1.3 fusion.6
  41.3 2.7 %copy.32 = bf16[2,512,8,128]{3,2,1,0:T(8,128)(2,1)} copy(bf16[2,512,8,128]{3,1,2,0:T(8,128)(2,1)S(1)} %convert_bitcast_fusion) | data formatting | bytes 4194304 | tf_op jit(solution)/shard_map/convert_element_type | solution.py:37
  44.0 11.6 %convert_bitcast_fusion.1 = bf16[2,512,8,128]{3,1,2,0:T(8,128)(2,1)} fusion(f32[2,8,512]{2,1,0:T(8,128)S(1)} %bitcast.63, f32[2,8,512,512]{2,3,1,0:T(8,128)} %get-tuple-element.10, f32[2,8,512]{2,1,0:T(8,128)S(1)} %get-tuple-element.9, bf16[2,512,8,128]{1,3,2,0:T(8,128)(2,1)} %bitcast.50, bf16[2,512,8,128]{1,3,2,0:T(8,128)(2,1)} %bitcast.52, ...), kind=kOutput, calls=%fused_computation.21 | convolution fusion | flops 2165309440 | bytes 25231360 | tf_op jit(solution)/shard_map/bhqk,bqhd->bkhd/dot_general | solution.py:44
  55.5 3.1 %copy.30 = bf16[2,512,8,128]{3,2,1,0:T(8,128)(2,1)S(1)} copy(bf16[2,512,8,128]{3,1,2,0:T(8,128)(2,1)} %convert_bitcast_fusion.1) | data formatting | bytes 4194304 | tf_op jit(solution)/shard_map/convert_element_type | solution.py:46
  58.7 0.0 copy-start.7
  58.7 2.4 %fusion.7 = f32[1024,1024]{1,0:T(8,128)S(1)} fusion(bf16[128,8,8,128]{3,2,1,0:T(8,128)(2,1)S(1)} %bitcast.60, bf16[1,1024,1024]{2,1,0:T(8,128)(2,1)S(1)} %copy-done), kind=kOutput, calls=%fused_computation.10 | convolution fusion | flops 2147483648 | bytes 8388608 | tf_op jit(solution)/shard_map/th,dh->td/dot_general | solution.py:54
  61.1 4.3 %fusion.17 = f32[1024,1024]{1,0:T(8,128)} fusion(f32[1024,1024]{1,0:T(8,128)S(1)} %fusion.7, bf16[1,1024,1024]{2,1,0:T(8,128)(2,1)S(1)} %copy-done.7, bf16[128,8,8,128]{3,2,1,0:T(8,128)(2,1)S(1)} %bitcast.62), kind=kOutput, calls=%fused_computation.22 | convolution fusion | flops 2148532224 | bytes 12582912 | tf_op jit(solution)/shard_map/th,dh->td/dot_general | solution.py:48
  65.3 0.0 reduce-scatter.3.cloned.1.call-update
  65.4 0.0 reduce-scatter.5.cloned.1.call-start
  65.4 52.8 %reduce-scatter.3.cloned.1.call-done = f32[2,512,128]{2,1,0:T(8,128)} async-done(((f32[2,512,1024]{2,1,0:T(8,128)}), f32[2,512,128]{2,1,0:T(8,128)}) %reduce-scatter.3.cloned.1.call-update) | async-done | bytes 524304 | tf_op jit(solution)/shard_map/reduce_scatter | solution.py:61
  118.2 0.0 reduce-scatter.5.cloned.1.call-update
  118.2 15.4 %reduce-scatter.5.cloned.1.call-done = f32[2,256,128]{2,1,0:T(8,128)} async-done(((f32[2,512,128]{2,1,0:T(8,128)}), f32[2,256,128]{2,1,0:T(8,128)}) %reduce-scatter.5.cloned.1.call-update) | async-done | bytes 262160 | tf_op jit(solution)/shard_map/reduce_scatter | solution.py:62
  133.6 1.2 multiply_reduce_fusion.1
  134.7 16.2 %psum.7 = f32[2,256]{1,0:T(2,128)S(1)} all-reduce(f32[2,256]{1,0:T(2,128)S(1)} %get-tuple-element.5), channel_id=1, replica_groups=mesh['section'=2,'tensor'=8,'dp'=2] {'tensor'}, use_global_device_ids=true, to_apply=%region_6.0 | all-reduce | flops 512 | bytes 4096 | tf_op jit(solution)/shard_map/psum | solution.py:20
  150.9 12.8 %all-gather.1 = f32[8,2,256]{2,1,0:T(2,128)S(1)} all-gather(f32[1,2,256]{2,1,0:T(2,128)S(1)} %bitcast.64), channel_id=2, replica_groups=mesh['section'=2,'tensor'=8,'dp'=2] {'tensor'}, dimensions={0}, use_global_device_ids=true | all-gather | bytes 18432 | tf_op jit(solution)/shard_map/all_gather | solution.py:65
  163.7 1.9 %multiply_subtract_fusion = f32[2,256,128]{2,1,0:T(8,128)} fusion(f32[2,256,128]{2,1,0:T(8,128)S(1)} %copy-done.5, f32[2,256,128]{2,1,0:T(8,128)} %reduce-scatter.5.cloned.1.call-done, f32[2,256]{1,0:T(2,128)S(1)} %get-tuple-element.8, f32[2,256]{1,0:T(2,128)S(1)} %get-tuple-element.7, f32[128]{0:T(128)S(1)} %copy-done.6), kind=kLoop, calls=%fused_computation.25 | loop fusion | flops 262144 | bytes 791040 | tf_op jit(solution)/shard_map/sub | solution.py:68
  (17 shorter events, 0.1 us)
Async XLA Ops:
  6.5 52.1 %copy-start = (bf16[1,1024,1024]{2,1,0:T(8,128)(2,1)S(1)}, bf16[1,1024,1024]{2,1,0:T(8,128)(2,1)}, u32[]{:S(2)}) copy-start(bf16[1,1024,1024]{2,1,0:T(8,128)(2,1)} %param.13) | copy-start | bytes 6291460
  6.5 111.6 %reduce-scatter.3.cloned.1.call-start = ((), (), s32[]{:S(2)}) async-start(), calls=%async_computation.2 | async-start | bytes 4718592 | tf_op jit(solution)/shard_map/reduce_scatter | solution.py:61
  6.5 3.7 %copy-start.3 = (bf16[1,2,512,1024]{3,2,1,0:T(8,128)(2,1)S(1)}, bf16[1,2,512,1024]{3,2,1,0:T(8,128)(2,1)}, u32[]{:S(2)}) copy-start(bf16[1,2,512,1024]{3,2,1,0:T(8,128)(2,1)} %param.9) | copy-start | bytes 6291460
  30.8 6.9 %copy-start.2 = (bf16[1,2,512,1024]{2,3,1,0:T(8,128)(2,1)S(1)}, bf16[1,2,512,1024]{2,3,1,0:T(8,128)(2,1)}, u32[]{:S(2)}) copy-start(bf16[1,2,512,1024]{2,3,1,0:T(8,128)(2,1)} %copy.21) | copy-start | bytes 6291460
  37.6 2.4 %copy-start.1 = (bf16[1,2,512,1024]{2,3,1,0:T(8,128)(2,1)S(1)}, bf16[1,2,512,1024]{2,3,1,0:T(8,128)(2,1)}, u32[]{:S(2)}) copy-start(bf16[1,2,512,1024]{2,3,1,0:T(8,128)(2,1)} %copy.39) | copy-start | bytes 6291460
  55.5 3.1 %copy-start.4 = (bf16[2,512,8,128]{3,2,1,0:T(8,128)(2,1)S(1)}, bf16[2,512,8,128]{3,2,1,0:T(8,128)(2,1)}, u32[]{:S(2)}) copy-start(bf16[2,512,8,128]{3,2,1,0:T(8,128)(2,1)} %copy.32) | copy-start | bytes 6291460
  58.7 2.4 %copy-start.7 = (bf16[1,1024,1024]{2,1,0:T(8,128)(2,1)S(1)}, bf16[1,1024,1024]{2,1,0:T(8,128)(2,1)}, u32[]{:S(2)}) copy-start(bf16[1,1024,1024]{2,1,0:T(8,128)(2,1)} %param.12) | copy-start | bytes 6291460
  65.3 68.2 %copy-start.5 = (f32[2,256,128]{2,1,0:T(8,128)S(1)}, f32[2,256,128]{2,1,0:T(8,128)}, u32[]{:S(2)}) copy-start(f32[2,256,128]{2,1,0:T(8,128)} %param.14) | copy-start | bytes 786436
  65.3 68.2 %copy-start.6 = (f32[128]{0:T(128)S(1)}, f32[128]{0:T(128)}, u32[]{:S(2)}) copy-start(f32[128]{0:T(128)} %param.15) | copy-start | bytes 1540
  65.4 68.2 %reduce-scatter.5.cloned.1.call-start = ((), (), s32[]{:S(2)}) async-start(), calls=%async_computation.3 | async-start | bytes 786432 | tf_op jit(solution)/shard_map/reduce_scatter | solution.py:62
Sparse Core Ops, SparseCore 0:
  65.5 52.6 reduce-scatter.2
  120.4 13.0 reduce-scatter.4
